TPU v7x, 32 devices: a whole 2x2x4 slice. The times are simulated.
32 devices in a mesh: gx: 8 (over y, x, core), gy: 4 (over z).
Axes of the slice: x: 2, y: 2, z: 4, core: 2. Of those that a mesh axis runs over, the one named last changes fastest.
Arguments:
- snapshots: bfloat16 [2, 1, 256, 256, 512], P(None, None, 'gx', 'gy'), may hold values from -12 to 12
- start: float32 [1, 32, 256, 256], P(None, None, 'gx', 'gy'), may hold values from -6 to 6
Outputs:
- basis_field: float32 [1, 32, 256, 256], P(None, None, 'gx', 'gy')
- phi: float32 [1, 2, 32, 32], replicated
All inputs are finite; a program needn't handle non-finite values.
Results may differ from a plain program's by a relative error of at most 0.0005.
Values may be sent and summed in bfloat16 or wider, within the bound.
A program may use at most 64 MiB of HBM per device.

v0:
```python
import jax
import jax.numpy as jnp
from jax import lax
from jax.sharding import PartitionSpec as P

ITERS = 4


precise = lax.Precision.HIGHEST


def swapped(x, axis, apart):
    return lax.ppermute(x, axis, [(i, i ^ 1 << apart) for i in range(lax.axis_size(axis))])


def passed_along(block, axis, distance):
    devices = range(lax.axis_size(axis))
    route = [(i - distance, i) for i in devices if i - distance in devices]
    return lax.ppermute(block, axis, route)


def inverse_factor(matrix):
    factor = jnp.linalg.cholesky(matrix)
    identity = jnp.broadcast_to(jnp.eye(matrix.shape[-1], dtype=matrix.dtype), matrix.shape)
    inverse = lax.linalg.triangular_solve(factor, identity, left_side=True, lower=True)
    return (factor, inverse)


def apply_inverse(inverse, right_side):
    return jnp.einsum("...kj,...jm->...km", inverse, right_side, precision=precise)


def shift_solve(inverse, right_matrix):
    inner = apply_inverse(inverse, right_matrix)
    return apply_inverse(jnp.swapaxes(inverse, -1, -2), inner)


def project(local_side):
    return lax.psum(local_side, ("gx", "gy"))


def gram_of(grown):
    return jnp.einsum("fkm,fjm->fkj", grown, grown, precision=precise)


def pair_grams(plus_terms, minus_terms):
    left_matrix = jnp.einsum("fkab,fjab->fkj", plus_terms, plus_terms, precision=precise)
    right_matrix = jnp.einsum("fkab,fjab->fkj", plus_terms, minus_terms, precision=precise)
    return (left_matrix, right_matrix)


def mirror_fields(stacked, rows, cols):
    moved = stacked
    for bit_number in range(lax.axis_size("gx").bit_length() - 1):
        moved = swapped(moved, "gx", bit_number)
    for bit_number in range(lax.axis_size("gy").bit_length() - 1):
        moved = swapped(moved, "gy", bit_number)
    lead = moved.shape[:-1]
    turned = moved.reshape(lead + (rows, cols))[..., ::-1, ::-1]
    return turned.reshape(moved.shape)


def shift_terms(field):
    rows = field.shape[2]
    cols = field.shape[3]
    below = passed_along(field[:, :, :1, :], "gx", -1)
    beside = passed_along(field[:, :, :, :1], "gy", -1)
    last_row_device = lax.axis_index("gx") == lax.axis_size("gx") - 1
    last_col_device = lax.axis_index("gy") == lax.axis_size("gy") - 1
    row_weight = jnp.where((jnp.arange(rows) == rows - 1) & last_row_device, 0.0, 1.0).astype(
        jnp.float32
    )
    col_weight = jnp.where((jnp.arange(cols) == cols - 1) & last_col_device, 0.0, 1.0).astype(
        jnp.float32
    )
    row_extended = jnp.concatenate([field, below], axis=2)
    col_extended = jnp.concatenate([field, beside], axis=3)
    row_plus = (row_extended[:, :, 1:] + row_extended[:, :, :-1]) * row_weight[:, None]
    row_minus = row_extended[:, :, 1:] - row_extended[:, :, :-1]
    col_plus = (col_extended[:, :, :, 1:] + col_extended[:, :, :, :-1]) * col_weight
    col_minus = col_extended[:, :, :, 1:] - col_extended[:, :, :, :-1]
    row_lhs, row_rhs = pair_grams(row_plus, row_minus)
    col_lhs, col_rhs = pair_grams(col_plus, col_minus)
    return (row_lhs, row_rhs, col_lhs, col_rhs)


def body(snapshots, start):
    frames, basis_count, rows, cols = start.shape
    upper_half = lax.axis_index("gx") < lax.axis_size("gx") // 2
    start_flat = start.reshape(frames, basis_count, rows * cols)
    own = snapshots.astype(jnp.float32).reshape(2, frames, rows * cols, -1)

    def local_side(weights, weights_mirror):
        p_real = jnp.einsum("fkm,fms->fks", weights, own[0], precision=precise)
        p_imag = jnp.einsum("fkm,fms->fks", weights, own[1], precision=precise)
        q_real = jnp.einsum("fkm,fms->fks", weights_mirror, own[0], precision=precise)
        q_imag = jnp.einsum("fkm,fms->fks", weights_mirror, own[1], precision=precise)
        first = jnp.where(upper_half, p_real - q_imag, p_imag + q_real)
        second = jnp.where(upper_half, -p_imag - q_real, p_real - q_imag)
        return jnp.concatenate([first, second], axis=-1)

    start_mirror = mirror_fields(start_flat[None], rows, cols)[0]
    basis = start_flat
    basis_mirror = start_mirror
    for step_index in range(ITERS):
        side = project(local_side(basis, basis_mirror))
        half = side.shape[-1] // 2
        side_first = side[..., :half]
        side_second = side[..., half:]
        g_real = jnp.einsum("fks,fms->fkm", side_first, own[0], precision=precise) - jnp.einsum(
            "fks,fms->fkm", side_second, own[1], precision=precise
        )
        g_imag = jnp.einsum("fks,fms->fkm", side_first, own[1], precision=precise) + jnp.einsum(
            "fks,fms->fkm", side_second, own[0], precision=precise
        )
        moved = mirror_fields(jnp.stack([g_real, g_imag]), rows, cols)
        grown = jnp.where(upper_half, g_real + moved[0], g_imag - moved[1])
        grown_mirror = jnp.where(upper_half, moved[1] - g_imag, moved[0] + g_real)
        grown, grown_mirror = (grown, grown_mirror)
        gram = lax.psum(gram_of(grown), ("gx", "gy"))
        factor, inverse = inverse_factor(gram)
        basis = apply_inverse(inverse, grown)
        basis_mirror = apply_inverse(inverse, grown_mirror)
    field = basis.reshape(frames, basis_count, rows, cols)
    local_terms = shift_terms(field)
    row_lhs, row_rhs, col_lhs, col_rhs = lax.psum(
        (local_terms[0], local_terms[1], local_terms[2], local_terms[3]), ("gx", "gy")
    )
    factors, inverses = inverse_factor(jnp.stack([row_lhs, col_lhs]))
    phi = jnp.swapaxes(shift_solve(inverses, jnp.stack([row_rhs, col_rhs])), 0, 1)
    return (field, phi)


def solution(mesh):
    return jax.shard_map(
        body,
        mesh=mesh,
        in_specs=(P(None, None, "gx", "gy", None), P(None, None, "gx", "gy")),
        out_specs=(P(None, None, "gx", "gy"), P()),
        check_vma=False,
    )
```

profile of v0, /device:TPU:0, one launch (start us, length us, event | category | flops | bytes accessed | tf_op | source)
XLA Modules:
  0.0 1151.9 jit_solution(10792632579092109949)
XLA Ops:
  10.2 2.8 collective-permute-start.1
  14.2 5.4 collective-permute-done.1
  21.4 2.6 fusion.107
  24.0 3.4 collective-permute-done.2
  30.0 4.3 collective-permute-done.3
  34.3 2.3 collective-permute-start.4
  37.7 9.2 collective-permute-done.4
  47.3 2.9 fusion.7
  50.2 2.9 select_bitcast_fusion.7
  53.8 125.1 %all-reduce.6.cloned.1.call-done = f32[1,32,1024]{2,1,0:T(8,128)} async-done(((f32[1,32,1024]{2,1,0:T(8,128)}), f32[1,32,1024]{2,1,0:T(8,128)}) %all-reduce.6.cloned.1.call-update) | async-done | bytes 131088 | tf_op jit(solution)/shard_map/psum | solution.py:39
  178.9 2.9 fusion.52
  181.8 1.9 fusion.51
  183.7 1.9 convolution_subtract_fusion.3
  185.6 1.9 convolution_add_fusion.3
  187.6 1.9 collective-permute-done.5
  191.0 12.5 %collective-permute-done.6 = f32[2,1,32,2048]{3,2,1,0:T(8,128)S(1)} collective-permute-done((f32[2,1,32,2048]{3,2,1,0:T(8,128)S(1)}, f32[2,1,32,2048]{3,2,1,0:T(8,128)S(1)}, u32[]{:S(2)}, u32[]{:S(2)}) %collective-permute-start.6) | collective-permute-done | bytes 524320 | tf_op jit(solution)/shard_map/ppermute | solution.py:13
  205.0 11.6 %collective-permute-done.7 = f32[2,1,32,2048]{3,2,1,0:T(8,128)S(1)} collective-permute-done((f32[2,1,32,2048]{3,2,1,0:T(8,128)S(1)}, f32[2,1,32,2048]{3,2,1,0:T(8,128)S(1)}, u32[]{:S(2)}, u32[]{:S(2)}) %collective-permute-start.7) | collective-permute-done | bytes 524320 | tf_op jit(solution)/shard_map/ppermute | solution.py:13
  218.1 10.8 collective-permute-done.8
  230.3 22.1 %collective-permute-done.9 = f32[2,1,32,2048]{3,2,1,0:T(8,128)S(1)} collective-permute-done((f32[2,1,32,2048]{3,2,1,0:T(8,128)S(1)}, f32[2,1,32,2048]{3,2,1,0:T(8,128)S(1)}, u32[]{:S(2)}, u32[]{:S(2)}) %collective-permute-start.9) | collective-permute-done | bytes 524320 | tf_op jit(solution)/shard_map/ppermute | solution.py:13
  259.4 38.3 %psum.85 = f32[1,32,32]{1,2,0:T(8,128)S(1)} all-reduce(f32[1,32,32]{1,2,0:T(8,128)S(1)} %convolution_bitcast_fusion.10), channel_id=1, replica_groups=mesh['gx'=8,'gy'=4] {'gx','gy'}, use_global_device_ids=true, to_apply=%region_1.2 | all-reduce | flops 1024 | bytes 8192 | tf_op jit(solution)/shard_map/psum | solution.py:120
  297.8 2.9 custom-call.21
  302.0 2.4 custom-call.22
  310.6 125.8 %all-reduce.8.cloned.1.call-done = f32[1,32,1024]{2,1,0:T(8,128)} async-done(((f32[1,32,1024]{2,1,0:T(8,128)}), f32[1,32,1024]{2,1,0:T(8,128)}) %all-reduce.8.cloned.1.call-update) | async-done | bytes 131088 | tf_op jit(solution)/shard_map/psum | solution.py:39
  436.4 2.9 fusion.54
  439.3 1.9 fusion.53
  441.2 1.9 convolution_subtract_fusion.2
  443.1 1.9 convolution_add_fusion.2
  445.1 1.9 collective-permute-done.10
  448.5 12.5 %collective-permute-done.11 = f32[2,1,32,2048]{3,2,1,0:T(8,128)S(1)} collective-permute-done((f32[2,1,32,2048]{3,2,1,0:T(8,128)S(1)}, f32[2,1,32,2048]{3,2,1,0:T(8,128)S(1)}, u32[]{:S(2)}, u32[]{:S(2)}) %collective-permute-start.11) | collective-permute-done | bytes 524320 | tf_op jit(solution)/shard_map/ppermute | solution.py:13
  462.5 11.6 %collective-permute-done.12 = f32[2,1,32,2048]{3,2,1,0:T(8,128)S(1)} collective-permute-done((f32[2,1,32,2048]{3,2,1,0:T(8,128)S(1)}, f32[2,1,32,2048]{3,2,1,0:T(8,128)S(1)}, u32[]{:S(2)}, u32[]{:S(2)}) %collective-permute-start.12) | collective-permute-done | bytes 524320 | tf_op jit(solution)/shard_map/ppermute | solution.py:13
  475.6 10.8 collective-permute-done.13
  487.8 22.1 %collective-permute-done.14 = f32[2,1,32,2048]{3,2,1,0:T(8,128)S(1)} collective-permute-done((f32[2,1,32,2048]{3,2,1,0:T(8,128)S(1)}, f32[2,1,32,2048]{3,2,1,0:T(8,128)S(1)}, u32[]{:S(2)}, u32[]{:S(2)}) %collective-permute-start.14) | collective-permute-done | bytes 524320 | tf_op jit(solution)/shard_map/ppermute | solution.py:13
  516.9 38.0 %psum.87 = f32[1,32,32]{1,2,0:T(8,128)S(1)} all-reduce(f32[1,32,32]{1,2,0:T(8,128)S(1)} %convolution_bitcast_fusion.9), channel_id=1, replica_groups=mesh['gx'=8,'gy'=4] {'gx','gy'}, use_global_device_ids=true, to_apply=%region_5.8 | all-reduce | flops 1024 | bytes 8192 | tf_op jit(solution)/shard_map/psum | solution.py:120
  555.0 2.9 custom-call.23
  559.2 2.4 custom-call.24
  567.8 125.8 %all-reduce.10.cloned.1.call-done = f32[1,32,1024]{2,1,0:T(8,128)} async-done(((f32[1,32,1024]{2,1,0:T(8,128)}), f32[1,32,1024]{2,1,0:T(8,128)}) %all-reduce.10.cloned.1.call-update) | async-done | bytes 131088 | tf_op jit(solution)/shard_map/psum | solution.py:39
  693.6 2.9 fusion.56
  696.5 1.9 fusion.55
  698.4 1.9 convolution_subtract_fusion.1
  700.3 1.9 convolution_add_fusion.1
  702.4 1.9 collective-permute-done.15
  705.7 12.5 %collective-permute-done.16 = f32[2,1,32,2048]{3,2,1,0:T(8,128)S(1)} collective-permute-done((f32[2,1,32,2048]{3,2,1,0:T(8,128)S(1)}, f32[2,1,32,2048]{3,2,1,0:T(8,128)S(1)}, u32[]{:S(2)}, u32[]{:S(2)}) %collective-permute-start.16) | collective-permute-done | bytes 524320 | tf_op jit(solution)/shard_map/ppermute | solution.py:13
  719.7 11.6 %collective-permute-done.17 = f32[2,1,32,2048]{3,2,1,0:T(8,128)S(1)} collective-permute-done((f32[2,1,32,2048]{3,2,1,0:T(8,128)S(1)}, f32[2,1,32,2048]{3,2,1,0:T(8,128)S(1)}, u32[]{:S(2)}, u32[]{:S(2)}) %collective-permute-start.17) | collective-permute-done | bytes 524320 | tf_op jit(solution)/shard_map/ppermute | solution.py:13
  732.8 10.8 collective-permute-done.18
  745.1 22.1 %collective-permute-done.19 = f32[2,1,32,2048]{3,2,1,0:T(8,128)S(1)} collective-permute-done((f32[2,1,32,2048]{3,2,1,0:T(8,128)S(1)}, f32[2,1,32,2048]{3,2,1,0:T(8,128)S(1)}, u32[]{:S(2)}, u32[]{:S(2)}) %collective-permute-start.19) | collective-permute-done | bytes 524320 | tf_op jit(solution)/shard_map/ppermute | solution.py:13
  774.1 38.1 %psum.89 = f32[1,32,32]{1,2,0:T(8,128)S(1)} all-reduce(f32[1,32,32]{1,2,0:T(8,128)S(1)} %convolution_bitcast_fusion.8), channel_id=1, replica_groups=mesh['gx'=8,'gy'=4] {'gx','gy'}, use_global_device_ids=true, to_apply=%region_7.10 | all-reduce | flops 1024 | bytes 8192 | tf_op jit(solution)/shard_map/psum | solution.py:120
  812.2 2.9 custom-call.25
  816.5 2.4 custom-call.26
  825.0 125.8 %all-reduce.12.cloned.1.call-done = f32[1,32,1024]{2,1,0:T(8,128)} async-done(((f32[1,32,1024]{2,1,0:T(8,128)}), f32[1,32,1024]{2,1,0:T(8,128)}) %all-reduce.12.cloned.1.call-update) | async-done | bytes 131088 | tf_op jit(solution)/shard_map/psum | solution.py:39
  950.9 2.9 fusion.58
  955.7 1.9 convolution_subtract_fusion
  957.6 1.9 convolution_add_fusion
  959.6 1.9 collective-permute-done.20
  963.0 12.5 %collective-permute-done.21 = f32[2,1,32,2048]{3,2,1,0:T(8,128)S(1)} collective-permute-done((f32[2,1,32,2048]{3,2,1,0:T(8,128)S(1)}, f32[2,1,32,2048]{3,2,1,0:T(8,128)S(1)}, u32[]{:S(2)}, u32[]{:S(2)}) %collective-permute-start.21) | collective-permute-done | bytes 524320 | tf_op jit(solution)/shard_map/ppermute | solution.py:13
  976.9 11.6 %collective-permute-done.22 = f32[2,1,32,2048]{3,2,1,0:T(8,128)S(1)} collective-permute-done((f32[2,1,32,2048]{3,2,1,0:T(8,128)S(1)}, f32[2,1,32,2048]{3,2,1,0:T(8,128)S(1)}, u32[]{:S(2)}, u32[]{:S(2)}) %collective-permute-start.22) | collective-permute-done | bytes 524320 | tf_op jit(solution)/shard_map/ppermute | solution.py:13
  990.1 10.8 collective-permute-done.23
  1002.3 22.0 %collective-permute-done.24 = f32[2,1,32,2048]{3,2,1,0:T(8,128)S(1)} collective-permute-done((f32[2,1,32,2048]{3,2,1,0:T(8,128)S(1)}, f32[2,1,32,2048]{3,2,1,0:T(8,128)S(1)}, u32[]{:S(2)}, u32[]{:S(2)}) %collective-permute-start.24) | collective-permute-done | bytes 524320 | tf_op jit(solution)/shard_map/ppermute | solution.py:13
  1026.3 38.1 %psum.91 = f32[1,32,32]{1,2,0:T(8,128)S(1)} all-reduce(f32[1,32,32]{1,2,0:T(8,128)S(1)} %convolution_bitcast_fusion.7), channel_id=1, replica_groups=mesh['gx'=8,'gy'=4] {'gx','gy'}, use_global_device_ids=true, to_apply=%region_9.12 | all-reduce | flops 1024 | bytes 8192 | tf_op jit(solution)/shard_map/psum | solution.py:120
  1064.5 2.9 custom-call.27
  1068.7 2.4 custom-call.28
  1076.0 12.2 %collective-permute-done.26 = f32[1,32,32,1]{3,1,2,0:T(8,128)S(1)} collective-permute-done((f32[1,32,32,1]{3,1,2,0:T(8,128)S(1)}, f32[1,32,32,1]{3,1,2,0:T(8,128)S(1)}, u32[]{:S(2)}, u32[]{:S(2)}) %collective-permute-start.26) | collective-permute-done | bytes 4128 | tf_op jit(solution)/shard_map/ppermute | solution.py:19
  1091.6 40.9 %all-reduce = (f32[1,1,32,32]{2,3,1,0:T(8,128)S(1)}, f32[1,1,32,32]{2,3,1,0:T(8,128)S(1)}, f32[1,1,32,32]{3,2,1,0:T(8,128)S(1)}, f32[1,1,32,32]{3,2,1,0:T(8,128)S(1)}) all-reduce(f32[1,1,32,32]{2,3,1,0:T(8,128)S(1)} %convolution_bitcast_fusion.5, ...), channel_id=1, replica_groups=mesh['gx'=8,'gy'=4] {'gx','gy'}, use_global_device_ids=true, to_apply=%region_10.13 | all-reduce | flops 4096 | bytes 32768 | tf_op jit(solution)/shard_map/psum | solution.py:126
  1132.6 5.9 custom-call.13
  1138.7 4.9 custom-call.14
  (175 shorter events, 93.1 us)
Async XLA Ops:
  7.2 171.7 %all-reduce.6.cloned.1.call-start = ((), (), s32[]{:S(2)}) async-start(), calls=%async_computation | async-start | bytes 262144 | tf_op jit(solution)/shard_map/psum | solution.py:39
  8.4 1.7 collective-permute-start
  10.2 9.5 collective-permute-start.1
  19.6 7.8 collective-permute-start.2
  24.0 13.7 %copy-start = (bf16[1,1,32,64,512]{4,3,2,1,0:T(8,128)(2,1)}, bf16[1,1,32,64,512]{4,3,2,1,0:T(8,128)(2,1)S(1)}, u32[]{:S(2)}) copy-start(bf16[1,1,32,64,512]{4,3,2,1,0:T(8,128)(2,1)S(1)} %get-tuple-element.15) | copy-start | bytes 6291460
  27.4 6.9 collective-permute-start.3
  34.3 12.6 %collective-permute-start.4 = (f32[1,1,32,2048]{3,2,1,0:T(8,128)S(1)}, f32[1,1,32,2048]{3,2,1,0:T(8,128)S(1)}, u32[]{:S(2)}, u32[]{:S(2)}) collective-permute-start(f32[1,1,32,2048]{3,2,1,0:T(8,128)S(1)} %collective-permute-done.3), channel_id=1, source_target_pairs={{0,2},{1,3},{2,0},{3,1},{4,6},{5,7},{6,4},{7,5},{8,10},{9,11},{10,... | collective-permute-start | bytes 786440 | tf_op jit(solution)/shard_map/ppermute | solution.py:13
  53.8 382.6 %all-reduce.8.cloned.1.call-start = ((), (), s32[]{:S(2)}) async-start(), calls=%async_computation.1 | async-start | bytes 262144 | tf_op jit(solution)/shard_map/psum | solution.py:39
  178.9 2.9 copy-start.1
  178.9 2.9 copy-start.8
  187.5 2.0 collective-permute-start.5
  189.5 14.0 %collective-permute-start.6 = (f32[2,1,32,2048]{3,2,1,0:T(8,128)S(1)}, f32[2,1,32,2048]{3,2,1,0:T(8,128)S(1)}, u32[]{:S(2)}, u32[]{:S(2)}) collective-permute-start(f32[2,1,32,2048]{3,2,1,0:T(8,128)S(1)} %collective-permute-done.5), channel_id=1, source_target_pairs={{0,8},{4,12},{8,0},{12,4},{16,24},{20,28},{24,16},{28,20},{1,9},{5... | collective-permute-start | bytes 1572872 | tf_op jit(solution)/shard_map/ppermute | solution.py:13
  203.5 13.1 %collective-permute-start.7 = (f32[2,1,32,2048]{3,2,1,0:T(8,128)S(1)}, f32[2,1,32,2048]{3,2,1,0:T(8,128)S(1)}, u32[]{:S(2)}, u32[]{:S(2)}) collective-permute-start(f32[2,1,32,2048]{3,2,1,0:T(8,128)S(1)} %collective-permute-done.6), channel_id=1, source_target_pairs={{0,16},{4,20},{8,24},{12,28},{16,0},{20,4},{24,8},{28,12},{1,17},{... | collective-permute-start | bytes 1572872 | tf_op jit(solution)/shard_map/ppermute | solution.py:13
  216.6 12.3 %collective-permute-start.8 = (f32[2,1,32,2048]{3,2,1,0:T(8,128)S(1)}, f32[2,1,32,2048]{3,2,1,0:T(8,128)S(1)}, u32[]{:S(2)}, u32[]{:S(2)}) collective-permute-start(f32[2,1,32,2048]{3,2,1,0:T(8,128)S(1)} %collective-permute-done.7), channel_id=1, source_target_pairs={{0,1},{1,0},{2,3},{3,2},{4,5},{5,4},{6,7},{7,6},{8,9},{9,8},{10,11... | collective-permute-start | bytes 1572872 | tf_op jit(solution)/shard_map/ppermute | solution.py:13
  228.8 23.5 %collective-permute-start.9 = (f32[2,1,32,2048]{3,2,1,0:T(8,128)S(1)}, f32[2,1,32,2048]{3,2,1,0:T(8,128)S(1)}, u32[]{:S(2)}, u32[]{:S(2)}) collective-permute-start(f32[2,1,32,2048]{3,2,1,0:T(8,128)S(1)} %collective-permute-done.8), channel_id=1, source_target_pairs={{0,2},{1,3},{2,0},{3,1},{4,6},{5,7},{6,4},{7,5},{8,10},{9,11},{10,... | collective-permute-start | bytes 1572872 | tf_op jit(solution)/shard_map/ppermute | solution.py:13
  304.7 1.8 copy-start.2
  310.5 383.1 %all-reduce.10.cloned.1.call-start = ((), (), s32[]{:S(2)}) async-start(), calls=%async_computation.2 | async-start | bytes 262144 | tf_op jit(solution)/shard_map/psum | solution.py:39
  436.4 2.9 copy-start.3
  436.4 2.9 copy-start.9
  445.1 2.0 collective-permute-start.10
  447.0 14.0 %collective-permute-start.11 = (f32[2,1,32,2048]{3,2,1,0:T(8,128)S(1)}, f32[2,1,32,2048]{3,2,1,0:T(8,128)S(1)}, u32[]{:S(2)}, u32[]{:S(2)}) collective-permute-start(f32[2,1,32,2048]{3,2,1,0:T(8,128)S(1)} %collective-permute-done.10), channel_id=1, source_target_pairs={{0,8},{4,12},{8,0},{12,4},{16,24},{20,28},{24,16},{28,20},{1,9},{5... | collective-permute-start | bytes 1572872 | tf_op jit(solution)/shard_map/ppermute | solution.py:13
  461.0 13.1 %collective-permute-start.12 = (f32[2,1,32,2048]{3,2,1,0:T(8,128)S(1)}, f32[2,1,32,2048]{3,2,1,0:T(8,128)S(1)}, u32[]{:S(2)}, u32[]{:S(2)}) collective-permute-start(f32[2,1,32,2048]{3,2,1,0:T(8,128)S(1)} %collective-permute-done.11), channel_id=1, source_target_pairs={{0,16},{4,20},{8,24},{12,28},{16,0},{20,4},{24,8},{28,12},{1,17},{... | collective-permute-start | bytes 1572872 | tf_op jit(solution)/shard_map/ppermute | solution.py:13
  474.1 12.3 %collective-permute-start.13 = (f32[2,1,32,2048]{3,2,1,0:T(8,128)S(1)}, f32[2,1,32,2048]{3,2,1,0:T(8,128)S(1)}, u32[]{:S(2)}, u32[]{:S(2)}) collective-permute-start(f32[2,1,32,2048]{3,2,1,0:T(8,128)S(1)} %collective-permute-done.12), channel_id=1, source_target_pairs={{0,1},{1,0},{2,3},{3,2},{4,5},{5,4},{6,7},{7,6},{8,9},{9,8},{10,11... | collective-permute-start | bytes 1572872 | tf_op jit(solution)/shard_map/ppermute | solution.py:13
  486.4 23.5 %collective-permute-start.14 = (f32[2,1,32,2048]{3,2,1,0:T(8,128)S(1)}, f32[2,1,32,2048]{3,2,1,0:T(8,128)S(1)}, u32[]{:S(2)}, u32[]{:S(2)}) collective-permute-start(f32[2,1,32,2048]{3,2,1,0:T(8,128)S(1)} %collective-permute-done.13), channel_id=1, source_target_pairs={{0,2},{1,3},{2,0},{3,1},{4,6},{5,7},{6,4},{7,5},{8,10},{9,11},{10,... | collective-permute-start | bytes 1572872 | tf_op jit(solution)/shard_map/ppermute | solution.py:13
  561.9 1.8 copy-start.4
  567.7 383.1 %all-reduce.12.cloned.1.call-start = ((), (), s32[]{:S(2)}) async-start(), calls=%async_computation.3 | async-start | bytes 262144 | tf_op jit(solution)/shard_map/psum | solution.py:39
  693.6 2.9 copy-start.5
  693.6 2.9 copy-start.10
  702.3 2.0 collective-permute-start.15
  704.3 14.0 %collective-permute-start.16 = (f32[2,1,32,2048]{3,2,1,0:T(8,128)S(1)}, f32[2,1,32,2048]{3,2,1,0:T(8,128)S(1)}, u32[]{:S(2)}, u32[]{:S(2)}) collective-permute-start(f32[2,1,32,2048]{3,2,1,0:T(8,128)S(1)} %collective-permute-done.15), channel_id=1, source_target_pairs={{0,8},{4,12},{8,0},{12,4},{16,24},{20,28},{24,16},{28,20},{1,9},{5... | collective-permute-start | bytes 1572872 | tf_op jit(solution)/shard_map/ppermute | solution.py:13
  718.2 13.1 %collective-permute-start.17 = (f32[2,1,32,2048]{3,2,1,0:T(8,128)S(1)}, f32[2,1,32,2048]{3,2,1,0:T(8,128)S(1)}, u32[]{:S(2)}, u32[]{:S(2)}) collective-permute-start(f32[2,1,32,2048]{3,2,1,0:T(8,128)S(1)} %collective-permute-done.16), channel_id=1, source_target_pairs={{0,16},{4,20},{8,24},{12,28},{16,0},{20,4},{24,8},{28,12},{1,17},{... | collective-permute-start | bytes 1572872 | tf_op jit(solution)/shard_map/ppermute | solution.py:13
  731.3 12.3 %collective-permute-start.18 = (f32[2,1,32,2048]{3,2,1,0:T(8,128)S(1)}, f32[2,1,32,2048]{3,2,1,0:T(8,128)S(1)}, u32[]{:S(2)}, u32[]{:S(2)}) collective-permute-start(f32[2,1,32,2048]{3,2,1,0:T(8,128)S(1)} %collective-permute-done.17), channel_id=1, source_target_pairs={{0,1},{1,0},{2,3},{3,2},{4,5},{5,4},{6,7},{7,6},{8,9},{9,8},{10,11... | collective-permute-start | bytes 1572872 | tf_op jit(solution)/shard_map/ppermute | solution.py:13
  743.6 23.5 %collective-permute-start.19 = (f32[2,1,32,2048]{3,2,1,0:T(8,128)S(1)}, f32[2,1,32,2048]{3,2,1,0:T(8,128)S(1)}, u32[]{:S(2)}, u32[]{:S(2)}) collective-permute-start(f32[2,1,32,2048]{3,2,1,0:T(8,128)S(1)} %collective-permute-done.18), channel_id=1, source_target_pairs={{0,2},{1,3},{2,0},{3,1},{4,6},{5,7},{6,4},{7,5},{8,10},{9,11},{10,... | collective-permute-start | bytes 1572872 | tf_op jit(solution)/shard_map/ppermute | solution.py:13
  819.2 1.8 copy-start.6
  950.9 2.9 copy-start.7
  950.9 2.9 copy-start.11
  959.5 2.0 collective-permute-start.20
  961.5 14.0 %collective-permute-start.21 = (f32[2,1,32,2048]{3,2,1,0:T(8,128)S(1)}, f32[2,1,32,2048]{3,2,1,0:T(8,128)S(1)}, u32[]{:S(2)}, u32[]{:S(2)}) collective-permute-start(f32[2,1,32,2048]{3,2,1,0:T(8,128)S(1)} %collective-permute-done.20), channel_id=1, source_target_pairs={{0,8},{4,12},{8,0},{12,4},{16,24},{20,28},{24,16},{28,20},{1,9},{5... | collective-permute-start | bytes 1572872 | tf_op jit(solution)/shard_map/ppermute | solution.py:13
  975.5 13.1 %collective-permute-start.22 = (f32[2,1,32,2048]{3,2,1,0:T(8,128)S(1)}, f32[2,1,32,2048]{3,2,1,0:T(8,128)S(1)}, u32[]{:S(2)}, u32[]{:S(2)}) collective-permute-start(f32[2,1,32,2048]{3,2,1,0:T(8,128)S(1)} %collective-permute-done.21), channel_id=1, source_target_pairs={{0,16},{4,20},{8,24},{12,28},{16,0},{20,4},{24,8},{28,12},{1,17},{... | collective-permute-start | bytes 1572872 | tf_op jit(solution)/shard_map/ppermute | solution.py:13
  988.6 12.3 %collective-permute-start.23 = (f32[2,1,32,2048]{3,2,1,0:T(8,128)S(1)}, f32[2,1,32,2048]{3,2,1,0:T(8,128)S(1)}, u32[]{:S(2)}, u32[]{:S(2)}) collective-permute-start(f32[2,1,32,2048]{3,2,1,0:T(8,128)S(1)} %collective-permute-done.22), channel_id=1, source_target_pairs={{0,1},{1,0},{2,3},{3,2},{4,5},{5,4},{6,7},{7,6},{8,9},{9,8},{10,11... | collective-permute-start | bytes 1572872 | tf_op jit(solution)/shard_map/ppermute | solution.py:13
  1000.8 23.5 %collective-permute-start.24 = (f32[2,1,32,2048]{3,2,1,0:T(8,128)S(1)}, f32[2,1,32,2048]{3,2,1,0:T(8,128)S(1)}, u32[]{:S(2)}, u32[]{:S(2)}) collective-permute-start(f32[2,1,32,2048]{3,2,1,0:T(8,128)S(1)} %collective-permute-done.23), channel_id=1, source_target_pairs={{0,2},{1,3},{2,0},{3,1},{4,6},{5,7},{6,4},{7,5},{8,10},{9,11},{10,... | collective-permute-start | bytes 1572872 | tf_op jit(solution)/shard_map/ppermute | solution.py:13
  1072.3 15.9 %collective-permute-start.26 = (f32[1,32,32,1]{3,1,2,0:T(8,128)S(1)}, f32[1,32,32,1]{3,1,2,0:T(8,128)S(1)}, u32[]{:S(2)}, u32[]{:S(2)}) collective-permute-start(f32[1,32,32,1]{3,1,2,0:T(8,128)S(1)} %bitcast.338), channel_id=1, source_target_pairs={{1,0},{2,1},{3,2},{5,4},{6,5},{7,6},{9,8},{10,9},{11,10},{13,12},{... | collective-permute-start | bytes 12296 | tf_op jit(solution)/shard_map/ppermute | solution.py:19
  1074.7 15.5 %collective-permute-start.25 = (f32[1,32,1,64]{3,1,2,0:T(8,128)S(1)}, f32[1,32,1,64]{3,1,2,0:T(8,128)S(1)}, u32[]{:S(2)}, u32[]{:S(2)}) collective-permute-start(f32[1,32,1,64]{3,1,2,0:T(8,128)S(1)} %slice.232), channel_id=1, source_target_pairs={{4,0},{8,4},{12,8},{16,12},{20,16},{24,20},{28,24},{5,1},{9,5},{13... | collective-permute-start | bytes 24584 | tf_op jit(solution)/shard_map/ppermute | solution.py:19
Sparse Core Ops, SparseCore 0:
  53.9 124.9 all-reduce.5
  310.6 125.7 all-reduce.7
  567.9 125.6 all-reduce.9
  825.1 125.6 all-reduce.11
where the time goes:
time: 1160 us; the launch traced here: 1150 us
  waiting for transfers between devices  774 us (67%)
  blocking collectives  193 us (17%)
  matrix products  65.3 us (6%)
  other arithmetic  40.8 us (4%)
  starting transfers between devices  35.6 us (3%)
  local copies, waits for them, and re-layouts  28.2 us (2%)
  between operations  15 us (1%)
    psum x4, waiting for transfers between devices, project(): return lax.psum(local_side, ('gx', 'gy'))  503 us
    ppermute x25, waiting for transfers between devices, swapped(): lax.ppermute(x, axis, [(i, i ^ 1 << apart) for i in range(lax.axis_size(a...  259 us
    psum x4, blocking collectives, body(): gram = lax.psum(gram_of(grown), ('gx', 'gy'))  152 us
    psum x1, blocking collectives, body(): lax.psum((local_terms[0], local_terms[1], local_terms[2], local_terms[3])...  40.9 us
    ppermute x25, starting transfers between devices, swapped(): lax.ppermute(x, axis, [(i, i ^ 1 << apart) for i in range(lax.axis_size(a...  32.9 us
  transfers between devices with their start and end apart: 31, of which 30 were waited for; matrix products, arithmetic and copies ran while one was open for 1% of the time, Pallas kernels for 0%

commit v1 on v0

v1 whole, which is shorter than its diff:
```python
import functools

import jax
import jax.numpy as jnp
from jax import lax
from jax.experimental import pallas as pl
from jax.experimental.pallas import tpu as pltpu
from jax.sharding import PartitionSpec as P

ITERS = 4
TILE = (8, 128)
MESH = pl.DeviceIdType.MESH

precise = lax.Precision.HIGHEST


def position():
    across = lax.axis_size("gy")
    return lax.axis_index("gx") * across + lax.axis_index("gy")


def device_of(index):
    across = lax.axis_size("gy")
    return (lax.div(index, across), lax.rem(index, across))


def device_count():
    return lax.axis_size("gx") * lax.axis_size("gy")


def enter():
    n = device_count()
    me = position()
    barrier = pltpu.get_barrier_semaphore()

    def greet(k, carry):
        pl.semaphore_signal(
            barrier, inc=1, device_id=device_of(lax.rem(me + k, n)), device_id_type=MESH
        )
        return carry

    lax.fori_loop(1, n, greet, 0)
    pl.semaphore_wait(barrier, n - 1)


def all_reduce(own, landed, total, gathered, send_a, recv_a, send_b, recv_b):
    n = device_count()
    me = position()
    tiles = own.shape[0]

    def scatter(k):
        owner = lax.rem(me + k, n)
        return owner, pltpu.make_async_remote_copy(
            src_ref=own.at[lax.rem(owner, tiles)],
            dst_ref=landed.at[k],
            send_sem=send_a.at[k],
            recv_sem=recv_a.at[k],
            device_id=device_of(owner),
            device_id_type=MESH,
        )

    def spread(k):
        return pltpu.make_async_remote_copy(
            src_ref=total,
            dst_ref=gathered.at[lax.rem(me, tiles)],
            send_sem=send_b.at[k],
            recv_sem=recv_b.at[k],
            device_id=device_of(lax.rem(me + k, n)),
            device_id_type=MESH,
        )

    def scatter_start(k, carry):
        owner, copy = scatter(k)
        if n == tiles:
            copy.start()
        else:
            pl.when(owner < tiles)(lambda: copy.start())
        return carry

    lax.fori_loop(1, n, scatter_start, 0)

    def add_and_spread():
        def add(k, value):
            scatter(k)[1].wait_recv()
            return value + landed[k]

        value = lax.fori_loop(1, n, add, own[lax.rem(me, tiles)])
        total[...] = value
        gathered[lax.rem(me, tiles)] = value

        def spread_start(k, carry):
            spread(k).start()
            return carry

        lax.fori_loop(1, n, spread_start, 0)

    if n == tiles:
        add_and_spread()
    else:
        pl.when(me < tiles)(add_and_spread)

    def finish(k, carry):
        owner, copy = scatter(k)
        source = lax.rem(me + n - k, n)
        if n == tiles:
            copy.wait_send()
            spread(k).wait_send()
            spread(k).wait_recv()
        else:
            pl.when(owner < tiles)(lambda: copy.wait_send())
            pl.when(me < tiles)(lambda: spread(k).wait_send())
            pl.when(source < tiles)(lambda: spread(k).wait_recv())
        return carry

    lax.fori_loop(1, n, finish, 0)


def thirds(x):
    high = x.astype(jnp.bfloat16)
    rest = x - high.astype(jnp.float32)
    middle = rest.astype(jnp.bfloat16)
    low = (rest - middle.astype(jnp.float32)).astype(jnp.bfloat16)
    return jnp.concatenate([high, middle, low], axis=0)


def fold(x):
    rows = x.shape[0] // 3
    return x[:rows] + (x[rows : 2 * rows] + x[2 * rows :])


def eliminate(grams):
    size = grams[0].shape[0]
    row_of = lax.broadcasted_iota(jnp.int32, (size, size), 0)
    col_of = lax.broadcasted_iota(jnp.int32, (size, size), 1)
    row_index = lax.broadcasted_iota(jnp.int32, (size, 1), 0)
    eye = (row_of == col_of).astype(jnp.float32)
    pairs = [(gram, eye) for gram in grams]
    for j in range(size):
        done = []
        for left, inverse in pairs:
            scale = lax.rsqrt(left[j : j + 1, j : j + 1])
            left_row = left[j : j + 1] * scale
            inverse_row = inverse[j : j + 1] * scale
            below = jnp.where(row_index > j, left[:, j : j + 1] * scale, 0.0)
            left = jnp.where(row_of == j, left_row, left - below * left_row)
            inverse = jnp.where(row_of == j, inverse_row, inverse - below * inverse_row)
            done.append((left, inverse))
        pairs = done
    return [(jnp.where(col_of >= row_of, left, 0.0), inverse) for left, inverse in pairs]


def times(a, b):
    return jnp.dot(a, b, precision=precise, preferred_element_type=jnp.float32)


def contracted(a, b, axes, precision=None):
    return lax.dot_general(
        a, b, ((axes, axes), ((), ())), precision=precision, preferred_element_type=jnp.float32
    )


def inner(a, b):
    rows = b.shape[0] // 3
    blocks = fold(contracted(a, b, (1,)))
    return blocks[:, :rows] + (blocks[:, rows : 2 * rows] + blocks[:, 2 * rows :])


def iterate_kernel(
    cols,
    x_hbm,
    start_ref,
    field_ref,
    phi_ref,
    x_raw,
    x_ref,
    acc_ref,
    mine,
    theirs,
    blocks,
    edge_row,
    edge_col,
    below_ref,
    beside_ref,
    own,
    landed,
    total,
    gathered,
    load_sem,
    send_p,
    recv_p,
    send_h,
    recv_h,
    send_a,
    recv_a,
    send_b,
    recv_b,
):
    count, sensors = start_ref.shape
    snaps = x_ref.shape[1] // 2
    chunk = mine.shape[2]
    chunks = sensors // chunk
    width = blocks.shape[2]
    parts = sensors // width
    n = device_count()
    mirror = device_of(n - 1 - position())
    upper = lax.axis_index("gx") < lax.axis_size("gx") // 2
    tile_rows, tile_cols = TILE
    across = 2 * snaps // tile_cols

    turn_row = lax.broadcasted_iota(jnp.int32, (width, width), 0)
    turn_col = lax.broadcasted_iota(jnp.int32, (width, width), 1)
    turn = (jnp.where(upper, turn_row, width - 1 - turn_row) == turn_col).astype(jnp.bfloat16)

    def part_of(b):
        return jnp.where(upper, b, parts - 1 - b)

    def turned(values):
        return fold(jnp.dot(thirds(values), turn, preferred_element_type=jnp.float32))

    load = pltpu.make_async_copy(x_hbm, x_raw, load_sem.at[0])
    load.start()
    enter()

    def exchange(c, first_row, here_row, rows):
        return pltpu.make_async_remote_copy(
            src_ref=mine.at[c, pl.ds(first_row, rows)],
            dst_ref=theirs.at[c, pl.ds(here_row, rows)],
            send_sem=send_p.at[c],
            recv_sem=recv_p.at[c],
            device_id=mirror,
            device_id_type=MESH,
        )

    per_chunk = chunk // width
    for c in range(chunks):
        for k in range(per_chunk):
            at = pl.multiple_of(part_of(c * per_chunk + k) * width, width)
            mine[c, :count, k * width : (k + 1) * width] = turned(start_ref[:, pl.ds(at, width)])
        exchange(c, 0, 0, count).start()
    load.wait()
    for b in range(parts):
        at = pl.multiple_of(part_of(b) * width, width)
        for h in range(2):
            x_ref[b * width : (b + 1) * width, h * snaps : (h + 1) * snaps] = jnp.dot(
                turn, x_raw[h, pl.ds(at, width), :], preferred_element_type=jnp.float32
            ).astype(jnp.bfloat16)

    def project(weights_of):
        acc = None
        for c in range(chunks):
            term = jnp.dot(
                thirds(weights_of(c)),
                x_ref[c * chunk : (c + 1) * chunk, :],
                preferred_element_type=jnp.float32,
            )
            acc = term if acc is None else acc + term
        both = fold(acc)
        acc_ref[:, :snaps] = both[:count, :snaps] + both[count:, snaps:]
        acc_ref[:, snaps:] = both[count:, :snaps] - both[:count, snaps:]

    def start_weights(c):
        exchange(c, 0, 0, count).wait()
        here = mine[c, :count]
        there = theirs[c, :count]
        return jnp.concatenate(
            [jnp.where(upper, here, there), jnp.where(upper, -there, here)], axis=0
        )

    def weights(c):
        exchange(c, 0, 0, 2 * count).wait()
        here = mine[c]
        there = theirs[c]
        return jnp.concatenate(
            [here[:count] + there[:count], here[count:] - there[count:]], axis=0
        )

    def reduced(values):
        per_row = values.shape[1] // tile_cols
        places = [
            (i, j) for i in range(values.shape[0] // tile_rows) for j in range(per_row)
        ]
        for t, (i, j) in enumerate(places):
            own[t] = values[
                i * tile_rows : (i + 1) * tile_rows, j * tile_cols : (j + 1) * tile_cols
            ]
        all_reduce(own, landed, total, gathered, send_a, recv_a, send_b, recv_b)
        return jnp.concatenate(
            [
                jnp.concatenate([gathered[i * per_row + j] for j in range(per_row)], axis=1)
                for i in range(values.shape[0] // tile_rows)
            ],
            axis=0,
        )

    def next_side():
        side = reduced(acc_ref[...])
        split = thirds(side)
        ((_, inverse),) = eliminate([inner(split, split)])
        return times(inverse, side)

    def grow(side, first_row, here_row, rows):
        side_first = side[:, :snaps]
        side_second = side[:, snaps:]
        stacked = thirds(
            jnp.concatenate(
                [
                    jnp.concatenate([side_first, -side_second], axis=1),
                    jnp.concatenate([side_second, side_first], axis=1),
                ],
                axis=0,
            )
        )
        for c in range(chunks):
            mine[c] = fold(contracted(stacked, x_ref[c * chunk : (c + 1) * chunk, :], (1,)))
            exchange(c, first_row, here_row, rows).start()

    project(start_weights)

    def step(index, carry):
        grow(next_side(), 0, 0, 2 * count)
        project(weights)
        return carry

    lax.fori_loop(0, ITERS - 1, step, 0)

    sent = pl.multiple_of(jnp.where(upper, count, 0), count)
    grow(next_side(), sent, 0, count)
    for c in range(chunks):
        exchange(c, sent, 0, count).wait()
        there = theirs[c, :count]
        here = jnp.where(upper, mine[c, :count] + there, mine[c, count:] - there)
        for k in range(per_chunk):
            blocks[c * per_chunk + k] = here[:, k * width : (k + 1) * width]
    grown = jnp.concatenate([turned(blocks[part_of(b)]) for b in range(parts)], axis=1)

    edge = edge_row.shape[1]
    sensor_of = lax.broadcasted_iota(jnp.int32, (edge_col.shape[1], sensors), 1)
    line_of = lax.broadcasted_iota(jnp.int32, (edge_col.shape[1], sensors), 0)
    take = (sensor_of == line_of * cols).astype(jnp.bfloat16)
    put = (sensor_of == line_of * cols + cols - 1).astype(jnp.bfloat16)
    split = thirds(grown)
    edge_row[...] = grown[:, :edge]
    edge_col[...] = fold(contracted(split, take, (1,)))
    gx, gy = lax.axis_index("gx"), lax.axis_index("gy")
    nx, ny = lax.axis_size("gx"), lax.axis_size("gy")
    halos = [
        pltpu.make_async_remote_copy(
            src_ref=source,
            dst_ref=target,
            send_sem=send_h.at[k],
            recv_sem=recv_h.at[k],
            device_id=where,
            device_id_type=MESH,
        )
        for k, (source, target, where) in enumerate(
            [
                (edge_row, below_ref, (lax.rem(gx + nx - 1, nx), gy)),
                (edge_col, beside_ref, (gx, lax.rem(gy + ny - 1, ny))),
            ]
        )
    ]
    for halo in halos:
        halo.start()
    sums = [inner(split, split)]
    lane = lax.broadcasted_iota(jnp.int32, (count, sensors), 1)
    lane_edge = lax.broadcasted_iota(jnp.int32, (count, edge), 1)
    shifted_row = pltpu.roll(grown, sensors - cols, 1)
    shifted_col = pltpu.roll(grown, sensors - 1, 1)
    for halo in halos:
        halo.wait()
    tail = jnp.where(
        lane_edge < edge - cols,
        shifted_row[:, sensors - edge :],
        pltpu.roll(below_ref[...], (edge - cols) % edge, 1),
    )
    next_row = (
        tail if sensors == edge else jnp.concatenate([shifted_row[:, : sensors - edge], tail], axis=1)
    )
    last_col = lax.rem(lane, cols) == cols - 1
    beside = fold(jnp.dot(thirds(beside_ref[...]), put, preferred_element_type=jnp.float32))
    next_col = jnp.where(last_col, beside, shifted_col)
    drop_row = (lane >= sensors - cols) & (gx == nx - 1)
    drop_col = last_col & (gy == ny - 1)
    for neighbour, drop in ((next_row, drop_row), (next_col, drop_col)):
        plus = thirds(jnp.where(drop, 0.0, neighbour + grown))
        minus = thirds(jnp.where(drop, 0.0, neighbour - grown))
        sums += [inner(plus, plus), inner(plus, minus)]
    spare = -len(sums) * count % tile_cols
    if spare:
        sums.append(jnp.zeros((count, spare), jnp.float32))
    sums = reduced(jnp.concatenate(sums, axis=1))
    gram, row_lhs, row_rhs, col_lhs, col_rhs = [
        sums[:, k * count : (k + 1) * count] for k in range(5)
    ]
    (upper_factor, inverse), (_, row_inverse), (_, col_inverse) = eliminate(
        [gram, row_lhs, col_lhs]
    )
    field_ref[...] = times(inverse, grown)
    for k, (half, right) in enumerate(((row_inverse, row_rhs), (col_inverse, col_rhs))):
        solved = contracted(half, times(half, right), (0,), precise)
        phi_ref[k] = contracted(times(upper_factor, solved), inverse, (1,), precise)


def dma(*shape):
    return pltpu.SemaphoreType.DMA(shape)


def iterated(x, start, cols):
    count, sensors = start.shape
    n = device_count()
    tiles = count * 2 * x.shape[2] // (TILE[0] * TILE[1])
    chunk = min(512, sensors)
    chunks = sensors // chunk
    width = min(256, chunk)
    edge = -(-cols // TILE[1]) * TILE[1]
    lines = -(-(sensors // cols) // TILE[1]) * TILE[1]
    vmem = pl.BlockSpec(memory_space=pltpu.VMEM)

    def held(*shape):
        return pltpu.VMEM(shape, jnp.float32)

    return pl.pallas_call(
        functools.partial(iterate_kernel, cols),
        out_shape=[
            jax.ShapeDtypeStruct(start.shape, jnp.float32),
            jax.ShapeDtypeStruct((2, count, count), jnp.float32),
        ],
        in_specs=[pl.BlockSpec(memory_space=pl.ANY), vmem],
        out_specs=[vmem, vmem],
        scratch_shapes=[
            pltpu.VMEM(x.shape, jnp.bfloat16),
            pltpu.VMEM((sensors, 2 * x.shape[2]), jnp.bfloat16),
            held(count, 2 * x.shape[2]),
            held(chunks, 2 * count, chunk),
            held(chunks, 2 * count, chunk),
            held(sensors // width, count, width),
            held(count, edge),
            held(count, lines),
            held(count, edge),
            held(count, lines),
            held(tiles, *TILE),
            held(n, *TILE),
            held(*TILE),
            held(tiles, *TILE),
            dma(1),
            dma(chunks),
            dma(chunks),
            dma(2),
            dma(2),
            dma(n),
            dma(n),
            dma(n),
            dma(n),
        ],
        compiler_params=pltpu.CompilerParams(
            collective_id=0, has_side_effects=True, vmem_limit_bytes=48 * 2**20
        ),
    )(x, start)


def body(snapshots, start):
    frames, count, rows, cols = start.shape
    snaps = snapshots.shape[-1]
    fields = []
    phis = []
    for frame in range(frames):
        field, phi = iterated(
            snapshots[:, frame].reshape(2, rows * cols, snaps),
            start[frame].reshape(count, rows * cols),
            cols,
        )
        fields.append(field.reshape(count, rows, cols))
        phis.append(phi)
    return (jnp.stack(fields), jnp.stack(phis))


def solution(mesh):
    return jax.shard_map(
        body,
        mesh=mesh,
        in_specs=(P(None, None, "gx", "gy", None), P(None, None, "gx", "gy")),
        out_specs=(P(None, None, "gx", "gy"), P()),
        check_vma=False,
    )
```

time: 1160 us -> 197 us (0.17)
  waiting for transfers between devices: 774 us -> 0 us
  blocking collectives: 193 us -> 0 us
  Pallas kernels: 0 us -> 191 us
  matrix products: 65.3 us -> 0 us
  other arithmetic: 40.8 us -> 0 us
  starting transfers between devices: 35.6 us -> 0 us
  local copies, waits for them, and re-layouts: 28.2 us -> 5.04 us
  between operations: 15 us -> 0.64 us
    psum x4 -> x0, waiting for transfers between devices: 503 us -> none  [project(): return lax.psum(local_side, ('gx', 'gy'))]
    ppermute x27 -> x0, waiting for transfers between devices: 271 us -> none  [the longest x25 259 us: swapped(): lax.ppermute(x, axis, [(i, i ^ 1 << apart) for i in range(lax.axis_size(a...]
    psum x5 -> x0, blocking collectives: 193 us -> none  [the longest x4 152 us: body(): gram = lax.psum(gram_of(grown), ('gx', 'gy'))]
    pallas_call x0 -> x1, Pallas kernels: none -> 191 us  [iterated(): pl.pallas_call(functools.partial(iterate_kernel, cols), out_shape=[jax.Sh...]
    dot_general x49 -> x0, matrix products: 64.1 us -> none  [the longest x4 11.5 us: body(): jnp.einsum('fks,fms->fkm', side_first, own[0], precision=precise)]
    another operation x31 -> x0, other arithmetic: 37.9 us -> none  [the longest x16 20.4 us: inverse_factor(): factor = jnp.linalg.cholesky(matrix)]
    ppermute x27 -> x0, starting transfers between devices: 35.4 us -> none  [the longest x25 32.9 us: swapped(): lax.ppermute(x, axis, [(i, i ^ 1 << apart) for i in range(lax.axis_size(a...]
    slice x22 -> x0, local copies, waits for them, and re-layouts: 15.8 us -> none  [the longest x20 13.2 us: body(): grown = jnp.where(upper_half, g_real + moved[0], g_imag - moved[1])]
  transfers between devices with their start and end apart: 31 -> 0, of which waited for: 30 -> 0; matrix products, arithmetic and copies ran while one was open for 1% -> 0% of each run, Pallas kernels for 0% -> 0%
where the time goes in v1:
time: 197 us; the launch traced here: 196 us
  Pallas kernels  191 us (97%)
  local copies, waits for them, and re-layouts  5.04 us (3%)
    pallas_call x1, Pallas kernels, iterated(): pl.pallas_call(functools.partial(iterate_kernel, cols), out_shape=[jax.Sh...  191 us

profile of v1, /device:TPU:0, one launch (start us, length us, event | category | flops | bytes accessed | tf_op | source)
XLA Modules:
  0.0 196.4 jit_solution(3675039739116865276)
XLA Ops:
  0.6 1.2 reshape_squeeze.7.start_ref
  1.9 0.0 copy-start
  1.9 2.2 %copy-done = bf16[2,1,32,64,512]{4,3,2,1,0:T(8,128)(2,1)S(1)} copy-done((bf16[2,1,32,64,512]{4,3,2,1,0:T(8,128)(2,1)S(1)}, bf16[2,1,32,64,512]{4,3,2,1,0:T(8,128)(2,1)}, u32[]{:S(2)}) %copy-start) | copy-done | bytes 4194328
  4.0 190.7 %shard_map.41 = (f32[32,2048]{1,0:T(8,128)S(1)}, f32[2,32,32]{2,1,0:T(8,128)S(1)}) custom-call(bf16[2,2048,512]{2,1,0:T(8,128)(2,1)S(1)} %bitcast.4, f32[32,2048]{1,0:T(8,128)S(1)} %reshape_squeeze.7.start_ref), custom_call_target="tpu_custom_call" | custom-call | tf_op jit(solution)/shard_map/pallas_call | solution.py:422
  194.7 1.0 stack_reshape.3
  195.7 0.6 copy.5
Async XLA Ops:
  1.9 2.2 %copy-start = (bf16[2,1,32,64,512]{4,3,2,1,0:T(8,128)(2,1)S(1)}, bf16[2,1,32,64,512]{4,3,2,1,0:T(8,128)(2,1)}, u32[]{:S(2)}) copy-start(bf16[2,1,32,64,512]{4,3,2,1,0:T(8,128)(2,1)} %param.2) | copy-start | bytes 12582916

commit v2 on v1

--- a/solution.py
+++ b/solution.py
@@ -77,14 +77,14 @@
             pl.when(owner < tiles)(lambda: copy.start())
         return carry
 
-    lax.fori_loop(1, n, scatter_start, 0)
+    lax.fori_loop(1, n, scatter_start, 0, unroll=n <= 32)
 
     def add_and_spread():
         def add(k, value):
             scatter(k)[1].wait_recv()
             return value + landed[k]
 
-        value = lax.fori_loop(1, n, add, own[lax.rem(me, tiles)])
+        value = lax.fori_loop(1, n, add, own[lax.rem(me, tiles)], unroll=n <= 32)
         total[...] = value
         gathered[lax.rem(me, tiles)] = value
 
@@ -92,7 +92,7 @@
             spread(k).start()
             return carry
 
-        lax.fori_loop(1, n, spread_start, 0)
+        lax.fori_loop(1, n, spread_start, 0, unroll=n <= 32)
 
     if n == tiles:
         add_and_spread()

time: 197 us -> 196 us (level)
  no operation moved by 1% of the time
where the time goes in v2:
time: 196 us
  Pallas kernels  190 us (97%)
  local copies, waits for them, and re-layouts  5.04 us (3%)
    pallas_call x1, Pallas kernels, iterated(): pl.pallas_call(functools.partial(iterate_kernel, cols), out_shape=[jax.Sh...  190 us

profile of v2, /device:TPU:0, one launch (start us, length us, event | category | flops | bytes accessed | tf_op | source)
XLA Modules:
  0.0 196.2 jit_solution(10042650658957923531)
XLA Ops:
  0.6 1.2 reshape_squeeze.7.start_ref
  1.9 0.0 copy-start
  1.9 2.2 %copy-done = bf16[2,1,32,64,512]{4,3,2,1,0:T(8,128)(2,1)S(1)} copy-done((bf16[2,1,32,64,512]{4,3,2,1,0:T(8,128)(2,1)S(1)}, bf16[2,1,32,64,512]{4,3,2,1,0:T(8,128)(2,1)}, u32[]{:S(2)}) %copy-start) | copy-done | bytes 4194328
  4.0 190.5 %shard_map.41 = (f32[32,2048]{1,0:T(8,128)S(1)}, f32[2,32,32]{2,1,0:T(8,128)S(1)}) custom-call(bf16[2,2048,512]{2,1,0:T(8,128)(2,1)S(1)} %bitcast.4, f32[32,2048]{1,0:T(8,128)S(1)} %reshape_squeeze.7.start_ref), custom_call_target="tpu_custom_call" | custom-call | tf_op jit(solution)/shard_map/pallas_call | solution.py:422
  194.5 1.0 stack_reshape.3
  195.5 0.6 copy.5
Async XLA Ops:
  1.9 2.2 %copy-start = (bf16[2,1,32,64,512]{4,3,2,1,0:T(8,128)(2,1)S(1)}, bf16[2,1,32,64,512]{4,3,2,1,0:T(8,128)(2,1)}, u32[]{:S(2)}) copy-start(bf16[2,1,32,64,512]{4,3,2,1,0:T(8,128)(2,1)} %param.2) | copy-start | bytes 12582916
